TPU v7x, 256 devices: a whole 4x4x8 slice. The times are simulated.
256 devices in a mesh: section: 4 (over y), node: 8 (over z), torus: 8 (over x, core).
Axes of the slice: x: 4, y: 4, z: 8, core: 2. Of those that a mesh axis runs over, the one named last changes fastest.
Arguments:
- act_in: bfloat16 [4, 2048, 7168], P('section', 'node', 'torus'), may hold values from -28 to 28
- next_in: bfloat16 [2048, 7168], P('node', 'torus'), may hold values from -42 to 42
- routes: int32 [2, 4, 2048, 2], P(None, 'section', 'node'), may hold values from 0 to 7, all different within a row; in each aligned block of 256 rows (0 to 255, 256 to 511, ..., all dimensions but the last counted through in order) at most 80 rows name the same one
- route_w: float32 [2, 4, 2048, 2], P(None, 'section', 'node'), may hold values from 0.2 to 1
- hist: float32 [4], P('section'), may hold values from 2 to 8
- gate_w: bfloat16 [4, 8, 7168, 1024], P('section', 'node', 'torus'), may hold values from -0.0625 to 0.0625
- up_w: bfloat16 [4, 8, 7168, 1024], P('section', 'node', 'torus'), may hold values from -0.0625 to 0.0625
- down_w: bfloat16 [4, 8, 1024, 7168], P('section', 'node', None, 'torus'), may hold values from -0.09375 to 0.09375
Outputs:
- act_out: bfloat16 [2, 4, 2048, 7168], P(None, 'section', 'node', 'torus')
- peak_out: float32 [4, 2], P('section')
Inputs may be any that keep to these rules, and one draw needn't show every extreme that they name: `routes`: each token names 2 different experts; within the 256 tokens of one index of node (aligned blocks of rows of one tick and layer) no expert is named more than 80 times, a bound that some block reaches.
All inputs are finite; a program needn't handle non-finite values.
Results may differ from a plain program's by a relative error of at most 0.012.
Values may be sent and summed in bfloat16 or wider, within the bound.
A program may use at most 64 MiB of HBM per device.

v0:
```python
import jax
import jax.numpy as jnp
from jax import lax
from jax.sharding import Mesh
from jax.sharding import PartitionSpec as P

TORUS = ("torus_0", "torus_1")
NODE_TORUS = ("node", "torus_0", "torus_1")


FP8_LIMIT = 448.0


def passed_along(value, axis, steps):
    count = lax.axis_size(axis)
    initial, last = (max(0, -steps), min(count, count - steps))
    return lax.ppermute(value, axis, [(source, source + steps) for source in range(initial, last)])


def from_everyone(x, axis):
    length = lax.axis_size(axis)
    return lax.all_to_all(jnp.broadcast_to(x[None], (length, *x.shape)), axis, 0, 0, tiled=True)


def over_copies(x, axis):
    everything = from_everyone(x, axis)
    return jnp.max(everything, axis=0)


def split_up(x, dim, length):
    before, after = (x.shape[:dim], x.shape[dim + 1 :])
    return jnp.moveaxis(x.reshape(*before, length, -1, *after), dim, 0)


def summed_on_arrival(x, axis, dim):
    length = lax.axis_size(axis)
    tiles = lax.all_to_all(split_up(x, dim, length), axis, 0, 0, tiled=True)
    return jnp.sum(tiles.astype(jnp.float32), axis=0)


def cut_rows(length, count):
    unit = 8 if length >= 8 * count else 1
    return [length // unit * k // count * unit for k in range(1, count)]


def gather_in_order(x, axes, turns):
    tiles = x[None]
    for k in turns:
        tiles = lax.all_gather(tiles, axes[k], axis=0, tiled=True)
    current = [lax.axis_size(axes[k]) for k in reversed(turns)]
    tiles = tiles.reshape(*current, *x.shape)
    turned = sorted(range(len(turns)), key=lambda place: turns[len(turns) - 1 - place])
    return tiles.transpose(*turned, *range(len(turns), tiles.ndim)).reshape(-1, *x.shape)


def laid_out(tiles, dim):
    tiles = jnp.moveaxis(tiles, 0, dim)
    dims = tiles.shape
    return tiles.reshape(*dims[:dim], dims[dim] * dims[dim + 1], *dims[dim + 2 :])


def gather_at_once(x, axes, dim):
    numbers = list(range(len(axes)))[::-1]
    split_at = x.shape.index(max(x.shape[:-1] or x.shape))
    edges = [0, *cut_rows(x.shape[split_at], len(axes)), x.shape[split_at]]
    finished = []
    for k, (start, end) in enumerate(zip(edges, edges[1:])):
        if end > start:
            share = lax.slice_in_dim(x, start, end, axis=split_at)
            finished.append(gather_in_order(share, axes, numbers[k:] + numbers[:k]))
    return laid_out(jnp.concatenate(finished, axis=split_at + 1), dim)


def shards(act_in, next_in, routes, route_w, hist, gate_w, up_w, down_w):
    tokens_here = act_in.shape[1]
    route_count = routes.shape[3]
    n_node = lax.axis_size("node")
    capacity = 5 * tokens_here * route_count // (4 * n_node)
    slot_count = n_node * capacity
    gate_mat = gate_w[0, 0]
    up_mat = up_w[0, 0]
    down_mat = down_w[0, 0]
    width_here = gate_mat.shape[0]
    section_now = lax.axis_index("section")
    stream = act_in[0]
    quant_scale = hist[0]
    outputs = []
    peak_list = []
    expert_ids = jnp.arange(n_node, dtype=jnp.int32)
    slot_ids = jnp.arange(slot_count, dtype=jnp.int32)
    for tick_index in range(routes.shape[0]):
        if tick_index > 0:
            passed = passed_along(outputs[-1], "section", 1)
            stream = jnp.where(section_now == 0, next_in, passed)
        stream_f32 = stream.astype(jnp.float32)
        group_peak = over_copies(jnp.max(jnp.abs(stream_f32)), NODE_TORUS)
        quantized = jnp.clip(stream_f32 * (FP8_LIMIT / quant_scale), -FP8_LIMIT, FP8_LIMIT).astype(
            jnp.bfloat16
        )
        dequant = quant_scale / FP8_LIMIT
        expert_of = routes[tick_index, 0]
        weight_of = route_w[tick_index, 0]
        pair_count = tokens_here * route_count
        hits = (expert_of.reshape(pair_count)[:, None] == expert_ids[None, :]).astype(jnp.int32)
        slot_rank = jnp.cumsum(hits, axis=0) - hits
        target = jnp.sum((slot_rank + expert_ids[None, :] * capacity) * hits, axis=1)
        pair_table = (target[:, None] == slot_ids[None, :]).astype(jnp.bfloat16)
        send_mat = jnp.sum(pair_table.reshape(tokens_here, route_count, slot_count), axis=1)
        outgoing = lax.dot_general(
            send_mat, quantized, (((0,), (0,)), ((), ())), preferred_element_type=jnp.float32
        )
        outgoing = outgoing.astype(jnp.bfloat16).reshape(n_node, capacity, width_here)
        arrived = lax.all_to_all(outgoing, "node", split_axis=0, concat_axis=0, tiled=True).reshape(
            slot_count, width_here
        )
        gate_part = lax.dot_general(
            gate_mat, arrived, (((0,), (1,)), ((), ())), preferred_element_type=jnp.float32
        )
        up_part = lax.dot_general(
            up_mat, arrived, (((0,), (1,)), ((), ())), preferred_element_type=jnp.float32
        )
        own_units = summed_on_arrival(
            jnp.stack([gate_part, up_part], axis=1).astype(jnp.bfloat16), TORUS, 0
        )
        gate_val = own_units[:, 0] * dequant
        up_val = own_units[:, 1] * dequant
        hidden_part = (jax.nn.silu(gate_val) * up_val).astype(jnp.bfloat16)
        hidden_all = gather_at_once(hidden_part, TORUS, 0)
        expert_out = lax.dot_general(
            hidden_all, down_mat, (((0,), (0,)), ((), ())), preferred_element_type=jnp.float32
        )
        back_in = expert_out.astype(jnp.bfloat16).reshape(n_node, capacity, width_here)
        results = lax.all_to_all(back_in, "node", split_axis=0, concat_axis=0, tiled=True)
        results = results.reshape(slot_count, width_here)
        picked = jnp.dot(pair_table, results, preferred_element_type=jnp.float32)
        picked = picked.reshape(tokens_here, route_count, width_here)
        branch = jnp.sum(picked * weight_of[:, :, None], axis=1)
        layer_out = (stream_f32 + branch).astype(jnp.bfloat16)
        outputs.append(layer_out)
        peak_list.append(group_peak)
        quant_scale = group_peak
    return (jnp.stack(outputs)[:, None], jnp.stack(peak_list)[None, :])


def solution(mesh):
    finer = Mesh(
        mesh.devices.reshape(mesh.shape["section"], mesh.shape["node"], 4, 2),
        ("section", "node", "torus_0", "torus_1"),
    )
    return jax.shard_map(
        shards,
        mesh=finer,
        in_specs=(
            P("section", "node", TORUS),
            P("node", TORUS),
            P(None, "section", "node", None),
            P(None, "section", "node", None),
            P("section"),
            P("section", "node", TORUS, None),
            P("section", "node", TORUS, None),
            P("section", "node", None, TORUS),
        ),
        out_specs=(P(None, "section", "node", TORUS), P("section", None)),
        check_vma=False,
    )
```

profile of v0, /device:TPU:1, one launch (start us, length us, event | category | flops | bytes accessed | tf_op | source)
XLA Modules:
  0.0 346.1 jit_solution(7636992980110555096)
XLA Ops:
  7.0 38.7 %all_to_all.42 = bf16[8,80,896]{2,1,0:T(8,128)(2,1)S(1)} all-to-all(bf16[8,80,896]{2,1,0:T(8,128)(2,1)S(1)} %bitcast.190), channel_id=1, replica_groups=mesh['section'=4,'node'=8,'torus_0'=4,'torus_1'=2] {'node'}, dimensions={0} | all-to-all | bytes 2293760 | tf_op jit(solution)/shard_map/all_to_all | solution.py:113
  53.0 6.2 %all-to-all-start.1 = ((bf16[8,128,2,640]{1,3,2,0:T(8,128)(2,1)}), bf16[8,128,2,640]{1,3,2,0:T(8,128)(2,1)}, u32[]{:S(2)}, u32[]{:S(2)}) async-start(bf16[8,128,2,640]{1,3,2,0:T(8,128)(2,1)} %pad_maximum_fusion), calls=%async_computation.1 | async-start | bytes 5242880 | tf_op jit(solution)/shard_map/all_to_all | solution.py:37
  59.2 31.9 %all-to-all-done.1 = bf16[8,128,2,640]{1,3,2,0:T(8,128)(2,1)} async-done(((bf16[8,128,2,640]{1,3,2,0:T(8,128)(2,1)}), bf16[8,128,2,640]{1,3,2,0:T(8,128)(2,1)}, u32[]{:S(2)}, u32[]{:S(2)}) %all-to-all-start.1) | async-done | bytes 2621472 | tf_op jit(solution)/shard_map/all_to_all | solution.py:37
  93.6 2.5 all-gather
  96.3 9.5 %all-gather.1 = bf16[256,640]{1,0:T(8,128)(2,1)S(1)} all-gather(bf16[64,640]{1,0:T(8,128)(2,1)S(1)} %copy.108), channel_id=3, replica_groups=mesh['section'=4,'node'=8,'torus_0'=4,'torus_1'=2] {'torus_0'}, dimensions={0}, use_global_device_ids=true | all-gather | bytes 409600 | tf_op jit(solution)/shard_map/all_gather | solution.py:49
  105.8 5.3 %all_gather.27 = bf16[8,64,640]{2,1,0:T(8,128)(2,1)S(1)} all-gather(bf16[4,64,640]{2,1,0:T(8,128)(2,1)S(1)} %bitcast.198), channel_id=1, replica_groups=mesh['section'=4,'node'=8,'torus_0'=4,'torus_1'=2] {'torus_1'}, dimensions={0}, use_global_device_ids=true | all-gather | bytes 983040 | tf_op jit(solution)/shard_map/all_gather | solution.py:49
  111.2 10.5 %all_gather.25 = bf16[8,64,640]{2,1,0:T(8,128)(2,1)S(1)} all-gather(bf16[2,64,640]{2,1,0:T(8,128)(2,1)S(1)} %bitcast.207), channel_id=1, replica_groups=mesh['section'=4,'node'=8,'torus_0'=4,'torus_1'=2] {'torus_0'}, dimensions={0}, use_global_device_ids=true | all-gather | bytes 819200 | tf_op jit(solution)/shard_map/all_gather | solution.py:49
  123.2 2.6 fusion.24
  125.7 3.7 %all-to-all-start.2 = ((bf16[8,80,896]{2,1,0:T(8,128)(2,1)}), bf16[8,80,896]{2,1,0:T(8,128)(2,1)S(1)}, u32[]{:S(2)}, u32[]{:S(2)}) async-start(bf16[8,80,896]{2,1,0:T(8,128)(2,1)} %bitcast.202), calls=%async_computation.2 | async-start | bytes 2293760 | tf_op jit(solution)/shard_map/all_to_all | solution.py:133
  129.5 28.5 %all-to-all-done.2 = bf16[8,80,896]{2,1,0:T(8,128)(2,1)S(1)} async-done(((bf16[8,80,896]{2,1,0:T(8,128)(2,1)}), bf16[8,80,896]{2,1,0:T(8,128)(2,1)S(1)}, u32[]{:S(2)}, u32[]{:S(2)}) %all-to-all-start.2) | async-done | bytes 1146912 | tf_op jit(solution)/shard_map/all_to_all | solution.py:133
  161.4 4.0 %collective-permute-start = (bf16[256,896]{1,0:T(8,128)(2,1)}, bf16[256,896]{1,0:T(8,128)(2,1)}, u32[]{:S(2)}, u32[]{:S(2)}) collective-permute-start(bf16[256,896]{1,0:T(8,128)(2,1)} %get-tuple-element.7), channel_id=1, source_target_pairs={{0,64},{64,128},{128,192},{1,65},{65,129},{129,193},{2,66},{66,130... | collective-permute-start | bytes 1376264 | tf_op jit(solution)/shard_map/ppermute | solution.py:17
  166.9 7.5 %all-to-all-start.3 = ((f32[64,1,1]{2,1,0:T(1,128)}), f32[64,1,1]{2,1,0:T(1,128)S(1)}, u32[]{:S(2)}, u32[]{:S(2)}) async-start(f32[64,1,1]{2,1,0:T(1,128)} %broadcast_in_dim.18), calls=%async_computation.3 | async-start | bytes 65536 | tf_op jit(solution)/shard_map/all_to_all | solution.py:22
  174.6 9.3 %all-to-all-done.3 = f32[64,1,1]{2,1,0:T(1,128)S(1)} async-done(((f32[64,1,1]{2,1,0:T(1,128)}), f32[64,1,1]{2,1,0:T(1,128)S(1)}, u32[]{:S(2)}, u32[]{:S(2)}) %all-to-all-start.3) | async-done | bytes 288 | tf_op jit(solution)/shard_map/all_to_all | solution.py:22
  186.6 32.4 %all_to_all.43 = bf16[8,80,896]{2,1,0:T(8,128)(2,1)S(1)} all-to-all(bf16[8,80,896]{2,1,0:T(8,128)(2,1)S(1)} %bitcast.191), channel_id=1, replica_groups=mesh['section'=4,'node'=8,'torus_0'=4,'torus_1'=2] {'node'}, dimensions={0} | all-to-all | bytes 2293760 | tf_op jit(solution)/shard_map/all_to_all | solution.py:113
  225.0 6.0 %all-to-all-start.5 = ((bf16[8,128,2,640]{1,3,2,0:T(8,128)(2,1)}), bf16[8,128,2,640]{1,3,2,0:T(8,128)(2,1)}, u32[]{:S(2)}, u32[]{:S(2)}) async-start(bf16[8,128,2,640]{1,3,2,0:T(8,128)(2,1)} %pad_maximum_fusion.1), calls=%async_computation.5 | async-start | bytes 5242880 | tf_op jit(solution)/shard_map/all_to_all | solution.py:37
  231.6 31.3 %all-to-all-done.5 = bf16[8,128,2,640]{1,3,2,0:T(8,128)(2,1)} async-done(((bf16[8,128,2,640]{1,3,2,0:T(8,128)(2,1)}), bf16[8,128,2,640]{1,3,2,0:T(8,128)(2,1)}, u32[]{:S(2)}, u32[]{:S(2)}) %all-to-all-start.5) | async-done | bytes 2621472 | tf_op jit(solution)/shard_map/all_to_all | solution.py:37
  264.2 4.9 %all-to-all-start.7 = ((f32[64,1,1]{2,1,0:T(1,128)}), f32[64,1,1]{2,1,0:T(1,128)S(1)}, u32[]{:S(2)}, u32[]{:S(2)}) async-start(f32[64,1,1]{2,1,0:T(1,128)} %broadcast_in_dim.44), calls=%async_computation.7 | async-start | bytes 65536 | tf_op jit(solution)/shard_map/all_to_all | solution.py:22
  274.0 10.4 %all-gather.3 = bf16[256,640]{1,0:T(8,128)(2,1)S(1)} all-gather(bf16[64,640]{1,0:T(8,128)(2,1)S(1)} %copy.119), channel_id=5, replica_groups=mesh['section'=4,'node'=8,'torus_0'=4,'torus_1'=2] {'torus_0'}, dimensions={0}, use_global_device_ids=true | all-gather | bytes 409600 | tf_op jit(solution)/shard_map/all_gather | solution.py:49
  284.4 4.5 %all_gather.31 = bf16[8,64,640]{2,1,0:T(8,128)(2,1)S(1)} all-gather(bf16[4,64,640]{2,1,0:T(8,128)(2,1)S(1)} %bitcast.199), channel_id=1, replica_groups=mesh['section'=4,'node'=8,'torus_0'=4,'torus_1'=2] {'torus_1'}, dimensions={0}, use_global_device_ids=true | all-gather | bytes 983040 | tf_op jit(solution)/shard_map/all_gather | solution.py:49
  289.0 11.3 %all_gather.29 = bf16[8,64,640]{2,1,0:T(8,128)(2,1)S(1)} all-gather(bf16[2,64,640]{2,1,0:T(8,128)(2,1)S(1)} %bitcast.208), channel_id=1, replica_groups=mesh['section'=4,'node'=8,'torus_0'=4,'torus_1'=2] {'torus_0'}, dimensions={0}, use_global_device_ids=true | all-gather | bytes 819200 | tf_op jit(solution)/shard_map/all_gather | solution.py:49
  301.8 2.6 fusion.27
  304.3 6.9 %all-to-all-start.6 = ((bf16[8,80,896]{2,1,0:T(8,128)(2,1)}), bf16[8,80,896]{2,1,0:T(8,128)(2,1)}, u32[]{:S(2)}, u32[]{:S(2)}) async-start(bf16[8,80,896]{2,1,0:T(8,128)(2,1)} %bitcast.200), calls=%async_computation.6 | async-start | bytes 2293760 | tf_op jit(solution)/shard_map/all_to_all | solution.py:133
  315.0 27.6 %all-to-all-done.6 = bf16[8,80,896]{2,1,0:T(8,128)(2,1)} async-done(((bf16[8,80,896]{2,1,0:T(8,128)(2,1)}), bf16[8,80,896]{2,1,0:T(8,128)(2,1)}, u32[]{:S(2)}, u32[]{:S(2)}) %all-to-all-start.6) | async-done | bytes 1146912 | tf_op jit(solution)/shard_map/all_to_all | solution.py:133
  342.6 2.4 multiply_reduce_fusion
  (88 shorter events, 42.5 us)
Async XLA Ops:
  0.6 45.1 %copy-start = (bf16[1,1,896,1024]{3,2,1,0:T(8,128)(2,1)S(1)}, bf16[1,1,896,1024]{3,2,1,0:T(8,128)(2,1)}, u32[]{:S(2)}) copy-start(bf16[1,1,896,1024]{3,2,1,0:T(8,128)(2,1)} %param.14) | copy-start | bytes 5505028
  0.6 5.8 %copy-start.1 = (bf16[1,256,896]{2,1,0:T(8,128)(2,1)S(1)}, bf16[1,256,896]{2,1,0:T(8,128)(2,1)}, u32[]{:S(2)}) copy-start(bf16[1,256,896]{2,1,0:T(8,128)(2,1)} %param.8) | copy-start | bytes 1376260
  47.6 1.5 copy-start.5
  53.0 38.1 %all-to-all-start.1 = ((bf16[8,128,2,640]{1,3,2,0:T(8,128)(2,1)}), bf16[8,128,2,640]{1,3,2,0:T(8,128)(2,1)}, u32[]{:S(2)}, u32[]{:S(2)}) async-start(bf16[8,128,2,640]{1,3,2,0:T(8,128)(2,1)} %pad_maximum_fusion), calls=%async_computation.1 | async-start | bytes 5242880 | tf_op jit(solution)/shard_map/all_to_all | solution.py:37
  121.7 1.5 copy-start.7
  125.7 3.7 %copy-start.4 = (f32[2,1,256,2]{2,3,1,0:T(2,128)S(1)}, f32[2,1,256,2]{2,3,1,0:T(2,128)}, u32[]{:S(2)}) copy-start(f32[2,1,256,2]{2,3,1,0:T(2,128)} %param.11) | copy-start | bytes 12292
  125.7 32.2 %all-to-all-start.2 = ((bf16[8,80,896]{2,1,0:T(8,128)(2,1)}), bf16[8,80,896]{2,1,0:T(8,128)(2,1)S(1)}, u32[]{:S(2)}, u32[]{:S(2)}) async-start(bf16[8,80,896]{2,1,0:T(8,128)(2,1)} %bitcast.202), calls=%async_computation.2 | async-start | bytes 2293760 | tf_op jit(solution)/shard_map/all_to_all | solution.py:133
  159.0 0.9 copy-start.2
  159.9 25.4 %copy-start.3 = (bf16[256,896]{1,0:T(8,128)(2,1)S(1)}, bf16[256,896]{1,0:T(8,128)(2,1)}, u32[]{:S(2)}) copy-start(bf16[256,896]{1,0:T(8,128)(2,1)} %param.9) | copy-start | bytes 1376260
  161.4 23.9 %collective-permute-start = (bf16[256,896]{1,0:T(8,128)(2,1)}, bf16[256,896]{1,0:T(8,128)(2,1)}, u32[]{:S(2)}, u32[]{:S(2)}) collective-permute-start(bf16[256,896]{1,0:T(8,128)(2,1)} %get-tuple-element.7), channel_id=1, source_target_pairs={{0,64},{64,128},{128,192},{1,65},{65,129},{129,193},{2,66},{66,130... | collective-permute-start | bytes 1376264 | tf_op jit(solution)/shard_map/ppermute | solution.py:17
  166.9 17.0 %all-to-all-start.3 = ((f32[64,1,1]{2,1,0:T(1,128)}), f32[64,1,1]{2,1,0:T(1,128)S(1)}, u32[]{:S(2)}, u32[]{:S(2)}) async-start(f32[64,1,1]{2,1,0:T(1,128)} %broadcast_in_dim.18), calls=%async_computation.3 | async-start | bytes 65536 | tf_op jit(solution)/shard_map/all_to_all | solution.py:22
  219.0 1.6 copy-start.6
  225.0 38.0 %all-to-all-start.5 = ((bf16[8,128,2,640]{1,3,2,0:T(8,128)(2,1)}), bf16[8,128,2,640]{1,3,2,0:T(8,128)(2,1)}, u32[]{:S(2)}, u32[]{:S(2)}) async-start(bf16[8,128,2,640]{1,3,2,0:T(8,128)(2,1)} %pad_maximum_fusion.1), calls=%async_computation.5 | async-start | bytes 5242880 | tf_op jit(solution)/shard_map/all_to_all | solution.py:37
  264.2 40.1 %all-to-all-start.7 = ((f32[64,1,1]{2,1,0:T(1,128)}), f32[64,1,1]{2,1,0:T(1,128)S(1)}, u32[]{:S(2)}, u32[]{:S(2)}) async-start(f32[64,1,1]{2,1,0:T(1,128)} %broadcast_in_dim.44), calls=%async_computation.7 | async-start | bytes 65536 | tf_op jit(solution)/shard_map/all_to_all | solution.py:22
  300.3 1.5 copy-start.8
  304.3 38.3 %all-to-all-start.6 = ((bf16[8,80,896]{2,1,0:T(8,128)(2,1)}), bf16[8,80,896]{2,1,0:T(8,128)(2,1)}, u32[]{:S(2)}, u32[]{:S(2)}) async-start(bf16[8,80,896]{2,1,0:T(8,128)(2,1)} %bitcast.200), calls=%async_computation.6 | async-start | bytes 2293760 | tf_op jit(solution)/shard_map/all_to_all | solution.py:133
where the time goes:
time: 347 us; the launch traced here: 346 us
  waiting for transfers between devices  129 us (37%)
  blocking collectives  127 us (37%)
  starting transfers between devices  39.2 us (11%)
  other arithmetic  19 us (5%)
  matrix products  15.7 us (5%)
  local copies, waits for them, and re-layouts  13.1 us (4%)
    all_to_all x2, blocking collectives, shards(): lax.all_to_all(outgoing, 'node', split_axis=0, concat_axis=0, tiled=True)  71.1 us
    all_to_all x2, waiting for transfers between devices, summed_on_arrival(): tiles = lax.all_to_all(split_up(x, dim, length), axis, 0, 0, tiled=True)  63.2 us
    all_gather x8, blocking collectives, gather_in_order(): tiles = lax.all_gather(tiles, axes[k], axis=0, tiled=True)  56.2 us
    all_to_all x2, waiting for transfers between devices, shards(): lax.all_to_all(back_in, 'node', split_axis=0, concat_axis=0, tiled=True)  56.1 us
    all_to_all x2, starting transfers between devices, from_everyone(): lax.all_to_all(jnp.broadcast_to(x[None], (length, *x.shape)), axis, 0, 0,...  12.5 us
    all_to_all x2, starting transfers between devices, summed_on_arrival(): tiles = lax.all_to_all(split_up(x, dim, length), axis, 0, 0, tiled=True)  12.2 us
    all_to_all x2, starting transfers between devices, shards(): lax.all_to_all(back_in, 'node', split_axis=0, concat_axis=0, tiled=True)  10.6 us
    all_to_all x2, waiting for transfers between devices, from_everyone(): lax.all_to_all(jnp.broadcast_to(x[None], (length, *x.shape)), axis, 0, 0,...  9.32 us
  transfers between devices with their start and end apart: 7, of which 5 were waited for; matrix products, arithmetic and copies ran while one was open for 3% of the time, Pallas kernels for 0%

commit v1 on v0

v1 whole, which is shorter than its diff:
```python
import functools

import jax
import jax.numpy as jnp
from jax import lax
from jax.experimental import pallas as pl
from jax.experimental.pallas import tpu as pltpu
from jax.sharding import PartitionSpec as P

MESH = pl.DeviceIdType.MESH
FP8_LIMIT = 448.0
F32 = jnp.float32
BF16 = jnp.bfloat16


def source_tables(n_node):
    if n_node == 8:
        return ((0, 1, 6, 3), (7, 2, 5, 4))
    half = n_node // 2
    return (tuple(range(half)), tuple(range(half, n_node)))


def dot(a, b):
    return jnp.dot(a, b, preferred_element_type=F32)


def kernel(
    n_section, n_node, n_torus, capacity,
    act, nxt, lanes_e, rows_e, rows_w, hist, gate_hbm, up_hbm, down_hbm,
    out, peak_out,
    w_gate, w_up, w_down, quant, d_send, arrived, own_part, rs_send, rs_recv,
    hidden, r_send, results, combine_w, y_buf, pk_src, pk_node, pk_torus,
    s_w, s_wp, r_wp, s_d, r_d, s_rs, r_rs, s_h, r_h, s_r, r_r, s_y, r_y, s_pn, r_pn, s_pt, r_pt,
):
    ticks, tokens, width = out.shape
    n_x = n_torus // 2
    ffw = w_gate.shape[1]
    unit = ffw // n_x
    core_rel = source_tables(n_node)
    n_step = len(core_rel[0])
    where_rel = {rel: (c, k) for c in range(2) for k, rel in enumerate(core_rel[c])}

    sec = lax.axis_index("section")
    z = lax.axis_index("node")
    t = lax.axis_index("torus")
    x = t // 2
    c = t % 2
    mate = x * 2 + (1 - c)

    def rcopy(src, dst, ssem, rsem, node=None, torus=None, section=None):
        ids = {}
        if section is not None:
            ids["section"] = section
        if node is not None:
            ids["node"] = node
        if torus is not None:
            ids["torus"] = torus
        return pltpu.make_async_remote_copy(src, dst, ssem, rsem, device_id=ids, device_id_type=MESH)

    def arrival(ref, rsem):
        rcopy(ref, ref, s_y.at[0], rsem, torus=mate).wait_recv()

    late = []

    def sent(copy, when=None):
        copy.start()
        late.append((when, copy))

    lane0 = pl.multiple_of(c * width, 128)

    own_w = (
        (gate_hbm, w_gate.at[pl.ds(lane0, width), :]),
        (up_hbm, w_up.at[pl.ds(lane0, width), :]),
        (down_hbm, w_down.at[c]),
    )
    loads = [pltpu.make_async_copy(src, dst, s_w.at[i]) for i, (src, dst) in enumerate(own_w)]
    for load in loads:
        load.start()

    barrier = pltpu.get_barrier_semaphore()
    greeted = 0
    for step in range(1, n_node):
        for core in range(2):
            pl.semaphore_signal(barrier, 1, device_id={"node": (z + step) % n_node, "torus": x * 2 + core}, device_id_type=MESH)
            greeted += 1
    for step in range(1, n_torus):
        pl.semaphore_signal(barrier, 1, device_id={"torus": (t + step) % n_torus}, device_id_type=MESH)
        greeted += 1
    if n_section > 1:
        @pl.when(sec > 0)
        def _():
            pl.semaphore_signal(barrier, 1, device_id={"section": sec - 1}, device_id_type=MESH)

    def routing_key(tick):
        ids = lax.broadcasted_iota(jnp.int32, (16, tokens), 0)
        hit = jnp.zeros((16, tokens), jnp.bool_)
        for k in range(lanes_e.shape[1]):
            rel = (lanes_e[tick, k : k + 1, :] - z + n_node) % n_node
            hit = hit | (rel == ids)
        before = lax.broadcasted_iota(jnp.int32, (tokens, tokens), 0) < lax.broadcasted_iota(jnp.int32, (tokens, tokens), 1)
        rank = dot(hit.astype(F32).astype(BF16), before.astype(F32).astype(BF16))
        return jnp.where(hit, rank, -1.0)

    def combine_table(tick):
        lane = lax.broadcasted_iota(jnp.int32, (tokens, 128), 1)
        after = lax.broadcasted_iota(jnp.int32, (tokens, tokens), 1) < lax.broadcasted_iota(jnp.int32, (tokens, tokens), 0)
        marks = []
        for k in range(rows_e.shape[2]):
            rel = (rows_e[tick, :, k : k + 1] - z + n_node) % n_node
            marks.append(rel == lane)
        hit = functools.reduce(jnp.logical_or, marks)
        rank = dot(after.astype(F32).astype(BF16), hit.astype(F32).astype(BF16))
        place = rank + lane.astype(F32) * capacity
        slot = lax.broadcasted_iota(jnp.int32, (tokens, n_node * capacity), 1).astype(F32)
        table = jnp.zeros((tokens, n_node * capacity), F32)
        for k, mark in enumerate(marks):
            target = jnp.sum(jnp.where(mark, place, 0.0), axis=1, keepdims=True)
            table = table + jnp.where(slot == target, rows_w[tick, :, k : k + 1], 0.0)
        high = table.astype(BF16)
        combine_w[tick, 0] = high
        combine_w[tick, 1] = (table - high.astype(F32)).astype(BF16)

    def quantize(stream, scale):
        value = stream.astype(F32) * (FP8_LIMIT / scale)
        quant[...] = jnp.clip(value, -FP8_LIMIT, FP8_LIMIT).astype(BF16)

    def peak_begin(tick, stream):
        pk_src[tick, 0] = jnp.full((8, 128), jnp.max(jnp.abs(stream.astype(F32))), F32)
        for step in range(1, n_node):
            sent(rcopy(pk_src.at[tick, 0], pk_node.at[tick, step], s_pn.at[tick, step], r_pn.at[tick, step], node=(z + step) % n_node))

    def peak_middle(tick):
        top = pk_src[tick, 0]
        for step in range(1, n_node):
            arrival(pk_node.at[tick, step], r_pn.at[tick, step])
            top = jnp.maximum(top, pk_node[tick, step])
        pk_src[tick, 1] = top
        for step in range(1, n_torus):
            sent(rcopy(pk_src.at[tick, 1], pk_torus.at[tick, step], s_pt.at[tick, step], r_pt.at[tick, step], torus=(t + step) % n_torus))

    def peak_end(tick):
        top = pk_src[tick, 1]
        for step in range(1, n_torus):
            arrival(pk_torus.at[tick, step], r_pt.at[tick, step])
            top = jnp.maximum(top, pk_torus[tick, step])
        return jnp.max(top)

    order = [(-core_rel[core][k]) % n_node for k in range(n_step) for core in range(2)]

    def dispatch(tick, key):
        rank_row = lax.broadcasted_iota(jnp.int32, (capacity, tokens), 0).astype(F32)
        for step in order:
            pick = (rank_row == key[step : step + 1, :]).astype(F32).astype(BF16)
            block = dot(pick, quant[...]).astype(BF16)
            core, k = where_rel[(-step) % n_node]
            target = arrived.at[tick, k, :, pl.ds(lane0, width)]
            if step:
                d_send[tick, step] = block
                sent(rcopy(d_send.at[tick, step], target, s_d.at[tick, step], r_d.at[tick, k, c], node=(z + step) % n_node, torus=x * 2 + core))
            else:
                @pl.when(c == core)
                def _():
                    arrived[tick, k, :, core * width : (core + 1) * width] = block

                @pl.when(c != core)
                def _():
                    d_send[tick, step] = block
                    rcopy(d_send.at[tick, step], target, s_d.at[tick, step], r_d.at[tick, k, c], torus=mate).start()

                late.append((c != core, rcopy(d_send.at[tick, step], target, s_d.at[tick, step], r_d.at[tick, k, c], torus=mate)))

    def stage_gate(tick, k):
        for half in range(2):
            def wait(half=half):
                arrival(arrived.at[tick, k, :, pl.ds(half * width, width)], r_d.at[tick, k, half])

            if where_rel[0] == (half, k):
                pl.when(c != half)(wait)
            else:
                wait()

        def body(j, carry):
            block = (x + 1 + j) % n_x
            cols = pl.ds(pl.multiple_of(block * unit, 128), unit)
            gate = dot(arrived[tick, k], w_gate[:, cols])
            up = dot(arrived[tick, k], w_up[:, cols])

            @pl.when(j < n_x - 1)
            def _():
                rs_send[tick, k, j, :, :unit] = gate.astype(BF16)
                rs_send[tick, k, j, :, unit:] = up.astype(BF16)
                rcopy(rs_send.at[tick, k, j], rs_recv.at[tick, k, j], s_rs.at[tick, k, j], r_rs.at[tick, k, j], torus=block * 2 + c).start()

            @pl.when(j == n_x - 1)
            def _():
                own_part[k, :, :unit] = gate
                own_part[k, :, unit:] = up

            return carry

        lax.fori_loop(0, n_x, body, 0)
        for j in range(n_x - 1):
            late.append((None, rcopy(rs_send.at[tick, k, j], rs_recv.at[tick, k, j], s_rs.at[tick, k, j], r_rs.at[tick, k, j], torus=((x + 1 + j) % n_x) * 2 + c)))

    def stage_hidden(tick, k, dequant):
        total = own_part[k]
        for j in range(n_x - 1):
            arrival(rs_recv.at[tick, k, j], r_rs.at[tick, k, j])
            total = total + rs_recv[tick, k, j].astype(F32)
        gate = total[:, :unit] * dequant
        up = total[:, unit:] * dequant
        cols = pl.ds(pl.multiple_of(x * unit, 128), unit)
        hidden[tick, k, :, cols] = (gate / (1.0 + jnp.exp(-gate)) * up).astype(BF16)
        for j in range(n_x - 1):
            place = hidden.at[tick, k, :, cols]
            sent(rcopy(place, place, s_h.at[tick, k, j], r_h.at[tick, k, j], torus=((x + 1 + j) % n_x) * 2 + c))

    def stage_down(tick, k):
        for j in range(n_x - 1):
            source = (x + 2 * n_x - 1 - j) % n_x
            arrival(hidden.at[tick, k, :, pl.ds(pl.multiple_of(source * unit, 128), unit)], r_h.at[tick, k, j])
        rel = jnp.where(c == 0, core_rel[0][k], core_rel[1][k])
        home = (z + rel) % n_node
        place = (n_node - rel) % n_node
        target = results.at[tick, pl.ds(pl.multiple_of(place * capacity, 16), capacity), :]
        core0, k0 = where_rel[0]
        for half in range(2):
            value = dot(hidden[tick, k], w_down[half]).astype(BF16)
            copy = rcopy(r_send.at[tick, k, half], target, s_r.at[tick, k, half], r_r.at[tick, place], node=home, torus=x * 2 + half)
            if k == k0 and half == core0:
                @pl.when(c == core0)
                def _():
                    results[tick, 0:capacity, :] = value

                @pl.when(c != core0)
                def _():
                    r_send[tick, k, half] = value
                    copy.start()

                late.append((c != core0, copy))
            else:
                r_send[tick, k, half] = value
                sent(copy)

    def stage_combine(tick, stream):
        core0, _k0 = where_rel[0]
        for place in range(n_node):
            def wait(place=place):
                arrival(results.at[tick, pl.ds(place * capacity, capacity), :], r_r.at[tick, place])

            if place == 0:
                pl.when(c != core0)(wait)
            else:
                wait()
        branch = dot(combine_w[tick, 0], results[tick]) + dot(combine_w[tick, 1], results[tick])
        out[tick] = (stream.astype(F32) + branch).astype(BF16)

    scale = hist[0]
    quantize(act[...], scale)
    key = routing_key(0)
    pl.semaphore_wait(barrier, greeted + jnp.where(sec < n_section - 1, 1, 0))
    dispatch(0, key)
    for i, load in enumerate(loads):
        load.wait()
        src, dst = own_w[i]
        sent(rcopy(dst, dst, s_wp.at[i], r_wp.at[i], torus=mate))
    peak_begin(0, act[...])
    combine_table(0)
    combine_table(1)

    schedule = []
    for k in range(n_step):
        schedule.append(("gate", k))
        if k >= 1:
            schedule.append(("hidden", k - 1))
        if k >= 2:
            schedule.append(("down", k - 2))
    schedule.append(("hidden", n_step - 1))
    if n_step >= 2:
        schedule.append(("down", n_step - 2))
    schedule.append(("down", n_step - 1))

    other = (
        w_gate.at[pl.ds(pl.multiple_of((1 - c) * width, 128), width), :],
        w_up.at[pl.ds(pl.multiple_of((1 - c) * width, 128), width), :],
        w_down.at[1 - c],
    )

    for tick in range(ticks):
        stream = act if tick == 0 else y_buf
        dequant = scale / FP8_LIMIT
        for kind, k in schedule:
            if kind == "gate":
                if tick == 0 and k == 0:
                    arrival(other[0], r_wp.at[0])
                    arrival(other[1], r_wp.at[1])
                stage_gate(tick, k)
                if k == 0:
                    peak_middle(tick)
            elif kind == "hidden":
                stage_hidden(tick, k, dequant)
            else:
                if tick == 0 and k == 0:
                    arrival(other[2], r_wp.at[2])
                stage_down(tick, k)
        peak = peak_end(tick)
        peak_out[0, tick] = peak
        stage_combine(tick, stream[...])
        if tick + 1 < ticks:
            scale = peak
            key = routing_key(tick + 1)
            if n_section > 1:
                @pl.when(sec < n_section - 1)
                def _():
                    rcopy(out.at[tick], y_buf, s_y.at[0], r_y.at[0], section=sec + 1).start()

                late.append((sec < n_section - 1, rcopy(out.at[tick], y_buf, s_y.at[0], r_y.at[0], section=sec + 1)))

                @pl.when(sec > 0)
                def _():
                    rcopy(out.at[tick], y_buf, s_y.at[0], r_y.at[0], section=sec - 1).wait_recv()

            @pl.when(sec == 0)
            def _():
                y_buf[...] = nxt[...]

            quantize(y_buf[...], scale)
            dispatch(tick + 1, key)
            peak_begin(tick + 1, y_buf[...])

    for when, copy in late:
        if when is None:
            copy.wait_send()
        else:
            pl.when(when)(copy.wait_send)


def solution(mesh):
    n_section, n_node, n_torus = (mesh.shape[a] for a in ("section", "node", "torus"))
    n_x = n_torus // 2

    def shards(act_in, next_in, routes, route_w, hist, gate_w, up_w, down_w):
        tokens, width = next_in.shape
        ticks, _, _, top = routes.shape
        capacity = 5 * tokens * top // (4 * n_node)
        ffw = gate_w.shape[3]
        unit = ffw // n_x
        n_step = n_node // 2
        lanes_e = routes[:, 0].transpose(0, 2, 1)
        rows_e = routes[:, 0]
        rows_w = route_w[:, 0]
        vmem = pl.BlockSpec(memory_space=pltpu.VMEM)
        hbm = pl.BlockSpec(memory_space=pl.ANY)
        smem = pl.BlockSpec(memory_space=pltpu.SMEM)
        dma = pltpu.SemaphoreType.DMA
        out, peak = pl.pallas_call(
            functools.partial(kernel, n_section, n_node, n_torus, capacity),
            out_shape=(
                jax.ShapeDtypeStruct((ticks, tokens, width), BF16),
                jax.ShapeDtypeStruct((1, ticks), F32),
            ),
            in_specs=[vmem, vmem, vmem, vmem, vmem, smem, hbm, hbm, hbm],
            out_specs=(vmem, smem),
            scratch_shapes=[
                pltpu.VMEM((2 * width, ffw), BF16),
                pltpu.VMEM((2 * width, ffw), BF16),
                pltpu.VMEM((2, ffw, width), BF16),
                pltpu.VMEM((tokens, width), BF16),
                pltpu.VMEM((ticks, n_node, capacity, width), BF16),
                pltpu.VMEM((ticks, n_step, capacity, 2 * width), BF16),
                pltpu.VMEM((n_step, capacity, 2 * unit), F32),
                pltpu.VMEM((ticks, n_step, max(1, n_x - 1), capacity, 2 * unit), BF16),
                pltpu.VMEM((ticks, n_step, max(1, n_x - 1), capacity, 2 * unit), BF16),
                pltpu.VMEM((ticks, n_step, capacity, ffw), BF16),
                pltpu.VMEM((ticks, n_step, 2, capacity, width), BF16),
                pltpu.VMEM((ticks, n_node * capacity, width), BF16),
                pltpu.VMEM((ticks, 2, tokens, n_node * capacity), BF16),
                pltpu.VMEM((tokens, width), BF16),
                pltpu.VMEM((ticks, 2, 8, 128), F32),
                pltpu.VMEM((ticks, n_node, 8, 128), F32),
                pltpu.VMEM((ticks, n_torus, 8, 128), F32),
                dma((3,)), dma((3,)), dma((3,)),
                dma((ticks, n_node)), dma((ticks, n_step, 2)),
                dma((ticks, n_step, max(1, n_x - 1))), dma((ticks, n_step, max(1, n_x - 1))),
                dma((ticks, n_step, max(1, n_x - 1))), dma((ticks, n_step, max(1, n_x - 1))),
                dma((ticks, n_step, 2)), dma((ticks, n_node)),
                dma((1,)), dma((1,)),
                dma((ticks, n_node)), dma((ticks, n_node)),
                dma((ticks, n_torus)), dma((ticks, n_torus)),
            ],
            compiler_params=pltpu.CompilerParams(collective_id=0, has_side_effects=True),
        )(act_in[0], next_in, lanes_e, rows_e, rows_w, hist, gate_w[0, 0], up_w[0, 0], down_w[0, 0])
        return out[:, None], peak

    return jax.shard_map(
        shards,
        mesh=mesh,
        in_specs=(
            P("section", "node", "torus"),
            P("node", "torus"),
            P(None, "section", "node", None),
            P(None, "section", "node", None),
            P("section"),
            P("section", "node", "torus", None),
            P("section", "node", "torus", None),
            P("section", "node", None, "torus"),
        ),
        out_specs=(P(None, "section", "node", "torus"), P("section", None)),
        check_vma=False,
    )
```

time: 347 us -> 173 us (0.50)
  the two profiles are of different devices: /device:TPU:1 before, /device:TPU:121 now
where the time goes in v1:
time: 173 us
  Pallas kernels  166 us (96%)
  local copies, waits for them, and re-layouts  5.76 us (3%)
    pallas_call x1, Pallas kernels, shards(): pl.pallas_call(functools.partial(kernel, n_section, n_node, n_torus, capa...  166 us
    unnamed x8, local copies, waits for them, and re-layouts  5.05 us

profile of v1, /device:TPU:121, one launch (start us, length us, event | category | flops | bytes accessed | tf_op | source)
XLA Modules:
  0.0 173.2 jit_solution(12261991891109219161)
XLA Ops:
  1.3 0.8 copy.10
  2.1 0.0 copy-start
  2.1 0.7 copy.12.lanes_e
  2.8 1.5 copy.11
  4.4 0.0 copy-done
  4.4 166.1 %shard_map.95 = (bf16[2,256,896]{2,1,0:T(8,128)(2,1)}, f32[1,2]{1,0:T(1,128)}) custom-call(bf16[256,896]{1,0:T(8,128)(2,1)} %bitcast.18, bf16[256,896]{1,0:T(8,128)(2,1)} %nxt.1, s32[2,2,256]{2,1,0:T(2,128)} %copy.12.lanes_e, s32[2,256,2]{2,1,0:T(8,128)} %bitcast.12, f32[2,256,2]{2,1,0:T(8,128)} %bitcast.16, f32[1]{0:T(128)S(6)} %copy.16.hist, ...), custom_call_target="tpu_custom_call" | custom-call | tf_op jit(solution)/shard_map/pallas_call | solution.py:356
  170.5 0.0 copy-start.1
  170.5 2.2 %copy.17 = bf16[2,1,256,896]{3,2,1,0:T(8,128)(2,1)} copy(bf16[2,1,256,896]{3,2,1,0:T(8,128)(2,1)} %bitcast.17) | data formatting | bytes 1835008
  172.7 0.0 copy-done.1
  172.7 0.5 copy.18
Async XLA Ops:
  2.1 2.3 %copy-start = (s32[2,1,256,2]{3,2,0,1:T(8,128)}, s32[2,1,256,2]{3,2,0,1:T(8,128)S(1)}, u32[]{:S(2)}) copy-start(s32[2,1,256,2]{3,2,0,1:T(8,128)S(1)} %copy.10) | copy-start | bytes 12292
  170.5 2.2 %copy-start.1 = (f32[1,2]{1,0:T(1,128)S(1)}, f32[1,2]{1,0:T(1,128)}, u32[]{:S(2)}) copy-start(f32[1,2]{1,0:T(1,128)} %get-tuple-element.11) | copy-start | bytes 28

commit v2 on v1

v2 whole, which is shorter than its diff:
```python
import functools

import jax
import jax.numpy as jnp
from jax import lax
from jax.experimental import pallas as pl
from jax.experimental.pallas import tpu as pltpu
from jax.sharding import PartitionSpec as P

MESH = pl.DeviceIdType.MESH
FP8_LIMIT = 448.0
F32 = jnp.float32
BF16 = jnp.bfloat16


PARTS = 3
LAG = 1
ORDER = (("gate", 0), ("gate", 1), ("hidden", 0), ("gate", 2), ("hidden", 1), ("down", 0),
         ("gate", 3), ("down", 1), ("hidden", 2), ("hidden", 3), ("down", 2), ("down", 3))
SCHEDULES = (ORDER, ORDER)


def PLAN(piece, places):
    if PARTS < 3 or len(places) < 8:
        return [(piece, places)]
    if piece == 0:
        return [(0, places)]
    if piece == 1:
        return [(1, places[:4])]
    return [(2, places[:4]), (1, places[4:6]), (2, places[4:6]), (1, places[6:]), (2, places[6:])]


def source_tables(n_node):
    if n_node == 8:
        return ((0, 1, 6, 3), (7, 2, 5, 4))
    half = n_node // 2
    return (tuple(range(half)), tuple(range(half, n_node)))


def column_cuts(width, parts):
    unit = width // 128
    parts = min(parts, unit)
    edges = [unit * i // parts * 128 for i in range(parts + 1)]
    return list(zip(edges, edges[1:]))


def dot(a, b):
    return jnp.dot(a, b, preferred_element_type=F32)


def kernel(
    n_section, n_node, n_torus, capacity,
    act, nxt, lanes_e, lanes_w, hist, gate_hbm, up_hbm, down_hbm,
    out, peak_out,
    w_gate, w_up, w_down, quant, d_send, arrived, own_part, rs_send, rs_recv,
    hidden, r_send, results, early_w, late_w, total_buf, y_buf, pk_src, pk_node, pk_torus,
    s_w, s_wp, r_wp, s_d, r_d, s_rs, r_rs, s_h, r_h, s_r, r_r, s_y, r_y, s_pn, r_pn, s_pt, r_pt,
):
    ticks, tokens, width = out.shape
    n_x = n_torus // 2
    ffw = w_gate.shape[1]
    unit = ffw // n_x
    core_rel = source_tables(n_node)
    n_step = len(core_rel[0])
    where_rel = {rel: (c, k) for c in range(2) for k, rel in enumerate(core_rel[c])}
    last = n_step - 1
    cuts = column_cuts(width, PARTS)
    places = [(-core_rel[core][k]) % n_node for k in range(n_step) for core in range(2)]
    position = {place: i for i, place in enumerate(places)}
    n_early = 2 * last
    whole = (0, width)

    sec = lax.axis_index("section")
    z = lax.axis_index("node")
    t = lax.axis_index("torus")
    x = t // 2
    c = t % 2
    mate = x * 2 + (1 - c)

    def rcopy(src, dst, ssem, rsem, node=None, torus=None, section=None):
        ids = {}
        if section is not None:
            ids["section"] = section
        if node is not None:
            ids["node"] = node
        if torus is not None:
            ids["torus"] = torus
        return pltpu.make_async_remote_copy(src, dst, ssem, rsem, device_id=ids, device_id_type=MESH)

    def arrival(ref, rsem):
        with jax.named_scope("wait"):
            rcopy(ref, ref, s_y.at[0], rsem, torus=mate).wait_recv()

    late = []

    def gone(ref, ssem, when=None):
        late.append((when, rcopy(ref, ref, ssem, r_y.at[0], torus=mate)))

    lane0 = pl.multiple_of(c * width, 128)

    own_w = (
        (gate_hbm, w_gate.at[pl.ds(lane0, width), :]),
        (up_hbm, w_up.at[pl.ds(lane0, width), :]),
        (down_hbm, w_down.at[c]),
    )
    loads = [pltpu.make_async_copy(src, dst, s_w.at[i]) for i, (src, dst) in enumerate(own_w)]
    for load in loads:
        load.start()

    barrier = pltpu.get_barrier_semaphore()
    greeted = 0
    for step in range(1, n_node):
        for core in range(2):
            pl.semaphore_signal(barrier, 1, device_id={"node": (z + step) % n_node, "torus": x * 2 + core}, device_id_type=MESH)
            greeted += 1
    for step in range(1, n_torus):
        pl.semaphore_signal(barrier, 1, device_id={"torus": (t + step) % n_torus}, device_id_type=MESH)
        greeted += 1
    if n_section > 1:
        @pl.when(sec > 0)
        def _():
            pl.semaphore_signal(barrier, 1, device_id={"section": sec - 1}, device_id_type=MESH)

    def routing_key(tick):
        ids = lax.broadcasted_iota(jnp.int32, (16, tokens), 0)
        hit = jnp.zeros((16, tokens), jnp.bool_)
        for k in range(lanes_e.shape[1]):
            rel = (lanes_e[tick, k : k + 1, :] - z + n_node) % n_node
            hit = hit | (rel == ids)
        before = lax.broadcasted_iota(jnp.int32, (tokens, tokens), 0) < lax.broadcasted_iota(jnp.int32, (tokens, tokens), 1)
        rank = dot(hit.astype(F32).astype(BF16), before.astype(F32).astype(BF16))
        return jnp.where(hit, rank, -1.0)

    def combine_table(tick):
        lane = lax.broadcasted_iota(jnp.int32, (tokens, 128), 1)
        after = lax.broadcasted_iota(jnp.int32, (tokens, tokens), 1) < lax.broadcasted_iota(jnp.int32, (tokens, tokens), 0)
        top = lanes_e.shape[1]
        rel = ((lanes_e[tick] - z + n_node) % n_node).astype(F32)
        rows = jnp.concatenate([rel, lanes_w[tick], jnp.zeros((128 - 2 * top, tokens), F32)], axis=0)
        turned = rows.T
        marks = [turned[:, k : k + 1] == lane.astype(F32) for k in range(top)]
        hit = functools.reduce(jnp.logical_or, marks)
        spot = dot(after.astype(F32).astype(BF16), hit.astype(F32).astype(BF16))
        for place, at in position.items():
            spot = spot + jnp.where(lane == place, F32(at * capacity), 0.0)
        slot = lax.broadcasted_iota(jnp.int32, (tokens, n_node * capacity), 1).astype(F32)
        table = jnp.zeros((tokens, n_node * capacity), F32)
        for k, mark in enumerate(marks):
            target = jnp.sum(jnp.where(mark, spot, 0.0), axis=1, keepdims=True)
            table = table + jnp.where(slot == target, turned[:, top + k : top + k + 1], 0.0)
        high = table.astype(BF16)
        low = (table - high.astype(F32)).astype(BF16)
        edge = n_early * capacity
        for i, part in enumerate((high, low)):
            early_w[tick, i] = part[:, :edge]
            late_w[tick, i] = part[:, edge:]

    def quantize(stream, scale, span):
        value = stream[:, span[0] : span[1]].astype(F32) * (FP8_LIMIT / scale)
        quant[:, span[0] : span[1]] = jnp.clip(value, -FP8_LIMIT, FP8_LIMIT).astype(BF16)

    def peak_begin(tick, stream):
        pk_src[tick, 0] = jnp.full((8, 128), jnp.max(jnp.abs(stream.astype(F32))), F32)
        for step in range(1, n_node):
            rcopy(pk_src.at[tick, 0], pk_node.at[tick, step], s_pn.at[tick], r_pn.at[tick], node=(z + step) % n_node).start()
        gone(pk_node.at[tick, 1:], s_pn.at[tick])

    def peak_middle(tick):
        top = pk_src[tick, 0]
        arrival(pk_node.at[tick, 1:], r_pn.at[tick])
        for step in range(1, n_node):
            top = jnp.maximum(top, pk_node[tick, step])
        pk_src[tick, 1] = top
        for step in range(1, n_torus):
            rcopy(pk_src.at[tick, 1], pk_torus.at[tick, step], s_pt.at[tick], r_pt.at[tick], torus=(t + step) % n_torus).start()
        gone(pk_torus.at[tick, 1:], s_pt.at[tick])

    def peak_end(tick):
        top = pk_src[tick, 1]
        arrival(pk_torus.at[tick, 1:], r_pt.at[tick])
        for step in range(1, n_torus):
            top = jnp.maximum(top, pk_torus[tick, step])
        return jnp.max(top)

    def spans_of_dispatch(tick):
        return [whole] if tick == 0 else cuts

    def spans_of_return(tick, k):
        return cuts if k == last and tick + 1 < ticks else [whole]

    def dispatch(tick, key, piece, steps=places):
        a, b = spans_of_dispatch(tick)[piece]
        rank_row = lax.broadcasted_iota(jnp.int32, (capacity, tokens), 0).astype(F32)
        for step in steps:
            pick = (rank_row == key[step : step + 1, :]).astype(F32).astype(BF16)
            block = dot(pick, quant[:, a:b]).astype(BF16)
            core, k = where_rel[(-step) % n_node]
            copy = rcopy(
                d_send.at[tick, step, :, a:b],
                arrived.at[tick, k, :, pl.ds(pl.multiple_of(lane0 + a, 128), b - a)],
                s_d.at[tick, 0 if step else 1], r_d.at[tick, k, c],
                node=(z + step) % n_node, torus=x * 2 + core if step else mate,
            )
            if step:
                d_send[tick, step, :, a:b] = block
                copy.start()
            else:
                @pl.when(c == core)
                def _():
                    arrived[tick, k, :, core * width + a : core * width + b] = block

                @pl.when(c != core)
                def _():
                    d_send[tick, step, :, a:b] = block
                    copy.start()

    def stage_gate(tick, k):
        if k == 0:
            gone(d_send.at[tick, 1:], s_d.at[tick, 0])
            gone(d_send.at[tick, 0], s_d.at[tick, 1], c != where_rel[0][0])
        for half in range(2):
            def wait(half=half):
                arrival(arrived.at[tick, k, :, half * width : (half + 1) * width], r_d.at[tick, k, half])

            if where_rel[0] == (half, k):
                pl.when(c != half)(wait)
            else:
                wait()

        def body(j, carry):
            block = (x + 1 + j) % n_x
            cols = pl.ds(pl.multiple_of(block * unit, 128), unit)
            gate = dot(arrived[tick, k], w_gate[:, cols])
            up = dot(arrived[tick, k], w_up[:, cols])

            @pl.when(j < n_x - 1)
            def _():
                rs_send[tick, k, j, :, :unit] = gate.astype(BF16)
                rs_send[tick, k, j, :, unit:] = up.astype(BF16)
                rcopy(rs_send.at[tick, k, j], rs_recv.at[tick, k, j], s_rs.at[tick], r_rs.at[tick, k], torus=block * 2 + c).start()

            @pl.when(j == n_x - 1)
            def _():
                own_part[k, :, :unit] = gate
                own_part[k, :, unit:] = up

            return carry

        with jax.named_scope(f"gatemm{tick}{k}"):
            lax.fori_loop(0, n_x, body, 0)
        if k == last and n_x > 1:
            gone(rs_send.at[tick], s_rs.at[tick])

    def stage_hidden(tick, k, dequant):
        total = own_part[k]
        if n_x > 1:
            arrival(rs_recv.at[tick, k], r_rs.at[tick, k])
        for j in range(n_x - 1):
            total = total + rs_recv[tick, k, j].astype(F32)
        gate = total[:, :unit] * dequant
        up = total[:, unit:] * dequant
        cols = pl.ds(pl.multiple_of(x * unit, 128), unit)
        hidden[tick, k, :, cols] = (gate / (1.0 + jnp.exp(-gate)) * up).astype(BF16)
        for j in range(n_x - 1):
            place = hidden.at[tick, k, :, cols]
            rcopy(place, place, s_h.at[tick], r_h.at[tick, k], torus=((x + 1 + j) % n_x) * 2 + c).start()
        if k == last and n_x > 1:
            gone(hidden.at[tick, :, :, : (n_x - 1) * unit], s_h.at[tick])

    def stage_down(tick, k):
        if n_x > 1:
            arrival(hidden.at[tick, k, :, : (n_x - 1) * unit], r_h.at[tick, k])
        home = (z + jnp.where(c == 0, core_rel[0][k], core_rel[1][k])) % n_node
        at = 2 * k + c
        core0, k0 = where_rel[0]
        spans = spans_of_return(tick, k)
        for piece, (a, b) in enumerate(spans):
            for half in range(2):
                value = dot(hidden[tick, k], w_down[half, :, a:b]).astype(BF16)
                own = k == k0 and half == core0
                if k == last:
                    ssem, rsem = s_r.at[tick, 2 + piece], r_r.at[tick, 2 + piece]
                else:
                    ssem = s_r.at[tick, 1 if own else 0]
                    rsem = r_r.at[tick, jnp.where(c == core0, 1, 0) if k == k0 else 0]
                copy = rcopy(
                    r_send.at[tick, k, half, :, a:b],
                    results.at[tick, pl.ds(pl.multiple_of(at * capacity, 16), capacity), a:b],
                    ssem, rsem, node=home, torus=x * 2 + half,
                )
                if own:
                    @pl.when(c == core0)
                    def _():
                        results[tick, 0:capacity, a:b] = value

                    @pl.when(c != core0)
                    def _():
                        r_send[tick, k, half, :, a:b] = value
                        copy.start()
                else:
                    r_send[tick, k, half, :, a:b] = value
                    copy.start()
            if k == last:
                gone(r_send.at[tick, k, :, :, a:b], s_r.at[tick, 2 + piece])
                if piece + 1 < len(spans):
                    late.pop()[1].wait_send()
        if k == last:
            gone(d_send.at[tick, : n_early - 1], s_r.at[tick, 0])
            gone(r_send.at[tick, k0, core0], s_r.at[tick, 1], c != core0)

    def results_in(tick, piece=None):
        if piece is None:
            arrival(results.at[tick, capacity : n_early * capacity, :], r_r.at[tick, 0])

            @pl.when(c != where_rel[0][0])
            def _():
                arrival(results.at[tick, 0:capacity, :], r_r.at[tick, 1])
        else:
            a, b = spans_of_return(tick, last)[piece]
            arrival(results.at[tick, n_early * capacity :, a:b], r_r.at[tick, 2 + piece])

    def combine_early(tick, stream):
        results_in(tick)
        rows = results[tick, : n_early * capacity, :]
        total_buf[...] = stream.astype(F32) + dot(early_w[tick, 0], rows) + dot(early_w[tick, 1], rows)

    def combine_late(tick, piece):
        a, b = spans_of_return(tick, last)[piece]
        results_in(tick, piece)
        rows = results[tick, n_early * capacity :, a:b]
        total = total_buf[:, a:b] + dot(late_w[tick, 0], rows) + dot(late_w[tick, 1], rows)
        out[tick, :, a:b] = total.astype(BF16)

    def relay(tick, piece):
        a, b = cuts[piece]
        return rcopy(out.at[tick, :, a:b], y_buf.at[:, a:b], s_y.at[0], r_y.at[piece], section=(sec + 1) % n_section)

    scale = hist[0]
    with jax.named_scope("start"):
        quantize(act, scale, whole)
        key = routing_key(0)
    with jax.named_scope("bar"):
      pl.semaphore_wait(barrier, greeted + jnp.where(sec < n_section - 1, 1, 0))
    peak_begin(0, act[...])
    with jax.named_scope("disp0"):
        dispatch(0, key, 0)
    for i, load in enumerate(loads):
        load.wait()
        src, dst = own_w[i]
        rcopy(dst, dst, s_wp.at[i], r_wp.at[i], torus=mate).start()
        gone(dst, s_wp.at[i])
    with jax.named_scope("tables"):
        combine_table(0)
        combine_table(1)

    def schedule_of(tick):
        if n_step == 4:
            return SCHEDULES[tick]
        return [(kind, k) for k in range(n_step) for kind in ("gate", "hidden", "down")]

    other = (
        w_gate.at[pl.ds(pl.multiple_of((1 - c) * width, 128), width), :],
        w_up.at[pl.ds(pl.multiple_of((1 - c) * width, 128), width), :],
        w_down.at[1 - c],
    )

    for tick in range(ticks):
        stream = act if tick == 0 else y_buf
        dequant = scale / FP8_LIMIT
        for kind, k in schedule_of(tick):
          with jax.named_scope(f"{kind}{tick}{k}"):
            if kind == "gate":
                if tick == 0 and k == 0:
                    arrival(other[0], r_wp.at[0])
                    arrival(other[1], r_wp.at[1])
                stage_gate(tick, k)
                if tick == 0 and k == last:
                    peak_middle(tick)
            elif kind == "hidden":
                stage_hidden(tick, k, dequant)
                if tick > 0 and k == last:
                    peak_middle(tick)
            else:
                if tick == 0 and k == 0:
                    arrival(other[2], r_wp.at[2])
                stage_down(tick, k)
        with jax.named_scope(f"peakend{tick}"):
            peak = peak_end(tick)
            peak_out[0, tick] = peak
        with jax.named_scope(f"early{tick}"):
            combine_early(tick, stream[...])
        if tick + 1 == ticks:
            with jax.named_scope(f"late{tick}"):
                combine_late(tick, 0)
            continue
        scale = peak
        key = routing_key(tick + 1)

        def pass_on(piece):
            with jax.named_scope(f"late{tick}{piece}"):
                combine_late(tick, piece)
            if n_section > 1:
                pl.when(sec < n_section - 1)(relay(tick, piece).start)

        def take_up(piece):
            a, b = cuts[piece]
            with jax.named_scope(f"waity{piece}"):
                if n_section > 1:
                    pl.when(sec > 0)(relay(tick, piece).wait_recv)

                @pl.when(sec == 0)
                def _():
                    y_buf[:, a:b] = nxt[:, a:b]

            with jax.named_scope(f"disp{piece}"):
                quantize(y_buf, scale, (a, b))
                for p, steps in PLAN(piece, places):
                    dispatch(tick + 1, key, p, steps)

        if n_section > 1:
            gone(out.at[tick], s_y.at[0], sec < n_section - 1)
        for piece in range(len(cuts)):
            pass_on(piece)
            if piece >= LAG:
                take_up(piece - LAG)
        for piece in range(max(0, len(cuts) - LAG), len(cuts)):
            take_up(piece)
        peak_begin(tick + 1, y_buf[...])

    with jax.named_scope("tail"):
        for when, copy in late:
            if when is None:
                copy.wait_send()
            else:
                pl.when(when)(copy.wait_send)


def solution(mesh):
    n_section, n_node, n_torus = (mesh.shape[a] for a in ("section", "node", "torus"))
    n_x = n_torus // 2

    def shards(act_in, next_in, routes, route_w, hist, gate_w, up_w, down_w):
        tokens, width = next_in.shape
        ticks, _, _, top = routes.shape
        capacity = 5 * tokens * top // (4 * n_node)
        ffw = gate_w.shape[3]
        unit = ffw // n_x
        n_step = n_node // 2
        lanes_e = routes[:, 0].transpose(0, 2, 1)
        lanes_w = route_w[:, 0].transpose(0, 2, 1)
        late_rows = 2 * capacity
        early_rows = (n_step - 1) * late_rows
        parts = len(column_cuts(width, PARTS))
        vmem = pl.BlockSpec(memory_space=pltpu.VMEM)
        hbm = pl.BlockSpec(memory_space=pl.ANY)
        smem = pl.BlockSpec(memory_space=pltpu.SMEM)
        dma = pltpu.SemaphoreType.DMA
        out, peak = pl.pallas_call(
            functools.partial(kernel, n_section, n_node, n_torus, capacity),
            out_shape=(
                jax.ShapeDtypeStruct((ticks, tokens, width), BF16),
                jax.ShapeDtypeStruct((1, ticks), F32),
            ),
            in_specs=[vmem, vmem, vmem, vmem, smem, hbm, hbm, hbm],
            out_specs=(vmem, smem),
            scratch_shapes=[
                pltpu.VMEM((2 * width, ffw), BF16),
                pltpu.VMEM((2 * width, ffw), BF16),
                pltpu.VMEM((2, ffw, width), BF16),
                pltpu.VMEM((tokens, width), BF16),
                pltpu.VMEM((ticks, n_node, capacity, width), BF16),
                pltpu.VMEM((ticks, n_step, capacity, 2 * width), BF16),
                pltpu.VMEM((n_step, capacity, 2 * unit), F32),
                pltpu.VMEM((ticks, n_step, max(1, n_x - 1), capacity, 2 * unit), BF16),
                pltpu.VMEM((ticks, n_step, max(1, n_x - 1), capacity, 2 * unit), BF16),
                pltpu.VMEM((ticks, n_step, capacity, ffw), BF16),
                pltpu.VMEM((ticks, n_step, 2, capacity, width), BF16),
                pltpu.VMEM((ticks, n_node * capacity, width), BF16),
                pltpu.VMEM((ticks, 2, tokens, early_rows), BF16),
                pltpu.VMEM((ticks, 2, tokens, late_rows), BF16),
                pltpu.VMEM((tokens, width), F32),
                pltpu.VMEM((tokens, width), BF16),
                pltpu.VMEM((ticks, 2, 8, 128), F32),
                pltpu.VMEM((ticks, n_node, 8, 128), F32),
                pltpu.VMEM((ticks, n_torus, 8, 128), F32),
                dma((3,)), dma((3,)), dma((3,)),
                dma((ticks, 2)), dma((ticks, n_step, 2)),
                dma((ticks,)), dma((ticks, n_step)),
                dma((ticks,)), dma((ticks, n_step)),
                dma((ticks, 2 + parts)), dma((ticks, 2 + parts)),
                dma((1,)), dma((parts,)),
                dma((ticks,)), dma((ticks,)), dma((ticks,)), dma((ticks,)),
            ],
            compiler_params=pltpu.CompilerParams(collective_id=0, has_side_effects=True),
        )(act_in[0], next_in, lanes_e, lanes_w, hist, gate_w[0, 0], up_w[0, 0], down_w[0, 0])
        return out[:, None], peak

    return jax.shard_map(
        shards,
        mesh=mesh,
        in_specs=(
            P("section", "node", "torus"),
            P("node", "torus"),
            P(None, "section", "node", None),
            P(None, "section", "node", None),
            P("section"),
            P("section", "node", "torus", None),
            P("section", "node", "torus", None),
            P("section", "node", None, "torus"),
        ),
        out_specs=(P(None, "section", "node", "torus"), P("section", None)),
        check_vma=False,
    )
```

time: 173 us -> 135 us (0.78)
  the two profiles are of different devices: /device:TPU:121 before, /device:TPU:41 now
where the time goes in v2:
time: 135 us
  Pallas kernels  131 us (97%)
  local copies, waits for them, and re-layouts  2.69 us (2%)
    pallas_call x1, Pallas kernels, shards(): pl.pallas_call(functools.partial(kernel, n_section, n_node, n_torus, capa...  131 us

profile of v2, /device:TPU:41, one launch (start us, length us, event | category | flops | bytes accessed | tf_op | source)
XLA Modules:
  0.0 134.9 jit_solution(17612873163307624127)
XLA Ops:
  1.3 130.9 %shard_map.95 = (bf16[2,256,896]{2,1,0:T(8,128)(2,1)}, f32[1,2]{1,0:T(1,128)}) custom-call(bf16[256,896]{1,0:T(8,128)(2,1)} %bitcast.17, bf16[256,896]{1,0:T(8,128)(2,1)} %nxt.1, s32[2,2,256]{2,1,0:T(2,128)} %bitcast.18, f32[2,2,256]{2,1,0:T(2,128)} %bitcast.19, f32[1]{0:T(128)S(6)} %copy.13.hist, bf16[896,1024]{1,0:T(8,128)(2,1)} %bitcast.13, ...), custom_call_target="tpu_custom_call" | custom-call | tf_op jit(solution)/shard_map/pallas_call | solution.py:458
  132.2 0.0 copy-start
  132.2 2.2 %copy.14 = bf16[2,1,256,896]{3,2,1,0:T(8,128)(2,1)} copy(bf16[2,1,256,896]{3,2,1,0:T(8,128)(2,1)} %bitcast.16) | data formatting | bytes 1835008
  134.4 0.0 copy-done
  134.4 0.5 copy.15
Async XLA Ops:
  132.2 2.2 %copy-start = (f32[1,2]{1,0:T(1,128)S(1)}, f32[1,2]{1,0:T(1,128)}, u32[]{:S(2)}) copy-start(f32[1,2]{1,0:T(1,128)} %get-tuple-element.11) | copy-start | bytes 28
